TPU v7x, 256 devices: a whole 4x4x8 slice. The times are simulated.
256 devices in a mesh: seq: 64 (over y, x_lo, z), dp: 4 (over x_hi, core).
Axes of the slice: x: 4 (x_hi: 2, x_lo: 2; x = x_hi * 2 + x_lo), y: 4, z: 8, core: 2. Of those that a mesh axis runs over, the one named last changes fastest.
Arguments:
- queries: bfloat16 [4, 16384, 2048], P('dp', 'seq'), may hold values from -12 to 12
- keys: bfloat16 [4, 16384, 1024], P('dp', 'seq'), may hold values from -6 to 6
- values: bfloat16 [4, 16384, 1024], P('dp', 'seq'), may hold values from -6 to 6
- out_grad: bfloat16 [4, 16384, 1792], P('dp', 'seq'), may hold values from -6 to 6
- out_weight: bfloat16 [2048, 1792], P('seq'), may hold values from -0.125 to 0.125
- seq_len: int32 [4], P('dp'), may hold values from 4096 to 16384, as said below
Outputs:
- query_grad: bfloat16 [4, 16384, 2048], P('dp', 'seq')
- key_grad: bfloat16 [4, 16384, 1024], P('dp', 'seq')
- value_grad: bfloat16 [4, 16384, 1024], P('dp', 'seq')
- weight_grad: float32 [2048, 1792], P('seq')
- grad_rms: float32 [], replicated
Inputs may be any that keep to these rules, and one draw needn't show every extreme that they name: `seq_len`: at least one sequence has the full length 16384.
All inputs are finite; a program needn't handle non-finite values.
Results may differ from a plain program's by a relative error of at most 0.014.
Values may be sent and summed in bfloat16 or wider, within the bound.
No kernel may reach another device: no remote copies, remote signals or barrier semaphores. Data moves between devices by JAX's collectives and lax.ppermute only.
A program may use at most 128 MiB of HBM per device.

v0:
```python
import functools
import jax
import jax.numpy as jnp
from jax import lax
from jax.sharding import Mesh
from jax.sharding import PartitionSpec as P

HEADS = 8
KV_HEADS = 4
HEAD_DIM = 256
D_OUT = 1792
WINDOW = 512
TOK_DEV = 256
SEQ = ("seq_0", "seq_1", "seq_2")
DP = ("dp_0", "dp_1")
SEQ_DP = ("seq_0", "seq_1", "seq_2", "dp_0", "dp_1")
SCALE = 0.0625
CAP = 50.0


def shifted(value, axis, steps):
    count = lax.axis_size(axis)
    initial, last = (max(0, -steps), min(count, count - steps))
    return lax.ppermute(value, axis, [(source, source + steps) for source in range(initial, last)])


def copy_for_each(value, axis):
    size = lax.axis_size(axis)
    return lax.all_to_all(
        jnp.broadcast_to(value[None], (size, *value.shape)), axis, 0, 0, tiled=True
    )


def taken_together(value, axis):
    everything = copy_for_each(value, axis)
    return jnp.sum(everything.astype(jnp.float32), axis=0)


def over_axes(value, axes):
    return functools.reduce(lax.psum, axes, value)


def band_block(q_rows, k_rows, v_rows, g_rows, q_pos, k_pos):
    count = q_rows.shape[0]
    span = k_rows.shape[0]
    group = HEADS // KV_HEADS
    qh = q_rows.reshape(count, KV_HEADS, group, HEAD_DIM)
    kh = k_rows.reshape(span, KV_HEADS, HEAD_DIM)
    vh = v_rows.reshape(span, KV_HEADS, HEAD_DIM)
    gh = g_rows.reshape(count, KV_HEADS, group, HEAD_DIM)
    raw = jnp.einsum("tkgd,jkd->kgtj", qh, kh, preferred_element_type=jnp.float32) * SCALE
    capped = CAP * jnp.tanh(raw / CAP)
    allowed = (
        (k_pos[None, :] >= 0)
        & (k_pos[None, :] <= q_pos[:, None])
        & (k_pos[None, :] > q_pos[:, None] - WINDOW)
    )
    expo = jnp.where(allowed, jnp.exp(capped), jnp.zeros((), jnp.float32))
    probs = expo / jnp.sum(expo, axis=-1, keepdims=True)
    probs_b = probs.astype(jnp.bfloat16)
    attn = jnp.einsum("kgtj,jkd->tkgd", probs_b, vh, preferred_element_type=jnp.float32).astype(
        jnp.bfloat16
    )
    delta = jnp.einsum("tkgd,tkgd->kgt", gh, attn, preferred_element_type=jnp.float32)[..., None]
    dprob = jnp.einsum("tkgd,jkd->kgtj", gh, vh, preferred_element_type=jnp.float32)
    dscore = (probs * (dprob - delta) * (1.0 - (capped / CAP) ** 2) * SCALE).astype(jnp.bfloat16)
    dq = jnp.einsum("kgtj,jkd->tkgd", dscore, kh, preferred_element_type=jnp.float32).reshape(
        count, -1
    )
    dk = jnp.einsum("kgtj,tkgd->jkd", dscore, qh, preferred_element_type=jnp.float32).reshape(
        span, -1
    )
    dv = jnp.einsum("kgtj,tkgd->jkd", probs_b, gh, preferred_element_type=jnp.float32).reshape(
        span, -1
    )
    return (dq, dk, dv, attn.reshape(count, -1))


def shards(queries, keys, values, out_grad, out_weight, seq_len):
    q_rows = queries[0]
    k_rows = keys[0]
    v_rows = values[0]
    length = seq_len[0]
    seq_devices = lax.axis_size(SEQ)
    rep_devices = lax.axis_size(DP)
    start = lax.axis_index(SEQ) * TOK_DEV
    positions = start + jnp.arange(TOK_DEV, dtype=jnp.int32)
    valid = positions < length
    masked = jnp.where(valid[:, None], out_grad[0], jnp.zeros((), jnp.bfloat16))
    grad_attn = lax.dot_general(
        masked,
        lax.all_gather(out_weight, SEQ, axis=0, tiled=True),
        (((1,), (1,)), ((), ())),
        preferred_element_type=jnp.float32,
    ).astype(jnp.bfloat16)
    reach = (WINDOW + TOK_DEV - 2) // TOK_DEV
    lead = reach * TOK_DEV
    key_parts = []
    val_parts = []
    for back in range(reach, 0, -1):
        earlier_k, earlier_v = shifted((k_rows, v_rows), SEQ, back)
        key_parts.append(earlier_k)
        val_parts.append(earlier_v)
    key_block = jnp.concatenate(key_parts + [k_rows], 0)
    val_block = jnp.concatenate(val_parts + [v_rows], 0)
    k_pos = start - lead + jnp.arange(lead + TOK_DEV, dtype=jnp.int32)
    dq_raw, dk_all, dv_all, attn = band_block(
        q_rows, key_block, val_block, grad_attn, positions, k_pos
    )
    dk_raw = dk_all[lead:]
    dv_raw = dv_all[lead:]
    for back in range(1, reach + 1):
        first = (reach - back) * TOK_DEV
        later_k, later_v = (
            shifted(dk_all[first : first + TOK_DEV].astype(jnp.bfloat16), SEQ, -back).astype(
                jnp.float32
            ),
            shifted(dv_all[first : first + TOK_DEV].astype(jnp.bfloat16), SEQ, -back).astype(
                jnp.float32
            ),
        )
        dk_raw = dk_raw + later_k
        dv_raw = dv_raw + later_v
    width = HEADS * HEAD_DIM
    part = lax.psum_scatter(
        lax.dot_general(attn, masked, (((0,), (0,)), ((), ())), preferred_element_type=jnp.float32),
        SEQ,
        scatter_dimension=0,
        tiled=True,
    )
    weight_raw = taken_together(part.astype(jnp.bfloat16), DP).astype(jnp.float32)
    weight_sq = jnp.sum(weight_raw * weight_raw) / rep_devices
    own_count = jnp.clip(length - start, 0, TOK_DEV)
    slots = TOK_DEV * seq_devices * rep_devices
    entries = slots * (HEADS + 2 * KV_HEADS) * HEAD_DIM + width * D_OUT
    act_sq = jnp.sum(dq_raw * dq_raw) + jnp.sum(dk_raw * dk_raw) + jnp.sum(dv_raw * dv_raw)
    total, act_total, weight_total = (
        over_axes(own_count.astype(jnp.float32), SEQ_DP),
        over_axes(act_sq, SEQ_DP),
        over_axes(weight_sq, SEQ_DP),
    )
    act_scale = slots / total
    weight_scale = lax.rsqrt(total)
    dq_s = dq_raw * act_scale
    dk_s = dk_raw * act_scale
    dv_s = dv_raw * act_scale
    squares = act_total * (act_scale * act_scale) + weight_total * (weight_scale * weight_scale)
    grad_rms = jnp.sqrt(squares / entries)
    weight_grad = weight_raw * weight_scale
    return (
        dq_s.astype(jnp.bfloat16)[None],
        dk_s.astype(jnp.bfloat16)[None],
        dv_s.astype(jnp.bfloat16)[None],
        weight_grad,
        grad_rms,
    )


def solution(mesh):
    split = Mesh(mesh.devices.reshape(4, 2, 8, 2, 2), ("seq_0", "seq_1", "seq_2", "dp_0", "dp_1"))
    placed = (
        P(DP, SEQ, None),
        P(DP, SEQ, None),
        P(DP, SEQ, None),
        P(DP, SEQ, None),
        P(SEQ, None),
        P(DP),
    )
    return jax.shard_map(
        shards,
        mesh=split,
        in_specs=placed,
        out_specs=(P(DP, SEQ, None), P(DP, SEQ, None), P(DP, SEQ, None), P(SEQ, None), P()),
        check_vma=False,
    )
```

profile of v0, /device:TPU:1, one launch (start us, length us, event | category | flops | bytes accessed | tf_op | source)
XLA Modules:
  0.0 783.0 jit_solution(6166765927309741051)
XLA Ops:
  9.2 5.2 collective-permute-start.3
  14.4 4.9 collective-permute-start.2
  20.5 5.6 collective-permute-start.1
  34.2 8.4 %collective-permute-done.2 = bf16[256,1024]{0,1:T(8,128)(2,1)} collective-permute-done((bf16[256,1024]{0,1:T(8,128)(2,1)S(1)}, bf16[256,1024]{0,1:T(8,128)(2,1)}, u32[]{:S(2)}, u32[]{:S(2)}) %collective-permute-start.2) | collective-permute-done | bytes 524320 | tf_op jit(solution)/shard_map/ppermute | solution.py:24
  44.6 22.7 %collective-permute-done.1 = bf16[256,1024]{0,1:T(8,128)(2,1)} collective-permute-done((bf16[256,1024]{0,1:T(8,128)(2,1)S(1)}, bf16[256,1024]{0,1:T(8,128)(2,1)}, u32[]{:S(2)}, u32[]{:S(2)}) %collective-permute-start.1) | collective-permute-done | bytes 524320 | tf_op jit(solution)/shard_map/ppermute | solution.py:24
  68.6 17.5 %collective-permute-done = bf16[256,1024]{0,1:T(8,128)(2,1)} collective-permute-done((bf16[256,1024]{0,1:T(8,128)(2,1)S(1)}, bf16[256,1024]{0,1:T(8,128)(2,1)}, u32[]{:S(2)}, u32[]{:S(2)}) %collective-permute-start) | collective-permute-done | bytes 524320 | tf_op jit(solution)/shard_map/ppermute | solution.py:24
  93.8 195.2 %all-gather.2.cloned.1.call-done = bf16[2048,1792]{1,0:T(8,128)(2,1)} async-done(((bf16[32,1792]{1,0:T(8,128)(2,1)}), bf16[2048,1792]{1,0:T(8,128)(2,1)}) %all-gather.2.cloned.1.call-update) | async-done | bytes 7340048 | tf_op jit(solution)/shard_map/all_gather | solution.py:92
  289.0 6.5 convolution_convert_fusion
  295.5 2.6 reshape.85
  298.1 3.3 bitcast_convert_fusion
  301.4 4.1 copy.91
  305.6 3.2 multiply_reduce_fusion
  308.8 7.4 fusion.6
  316.2 3.6 copy.76
  319.8 6.8 fusion.1
  337.1 3.9 fusion.28
  349.0 5.4 multiply_reduce_fusion.1
  354.3 302.3 %reduce-scatter.2.cloned.1.call-done = f32[32,1792]{1,0:T(8,128)} async-done(((f32[2048,1792]{1,0:T(8,128)}), f32[32,1792]{1,0:T(8,128)}) %reduce-scatter.2.cloned.1.call-update) | async-done | bytes 229392 | tf_op jit(solution)/shard_map/reduce_scatter | solution.py:125
  658.4 55.7 %all-to-all-start = ((bf16[4,32,1792]{2,1,0:T(8,128)(2,1)}), bf16[4,32,1792]{2,1,0:T(8,128)(2,1)S(1)}, u32[]{:S(2)}, u32[]{:S(2)}) async-start(bf16[4,32,1792]{2,1,0:T(8,128)(2,1)} %broadcast_in_dim.53), calls=%async_computation.1 | async-start | bytes 917504 | tf_op jit(solution)/shard_map/all_to_all | solution.py:29
  724.2 6.5 all-reduce.1
  730.7 4.4 all-reduce.4
  735.1 11.4 %all-reduce = (f32[]{:T(128)}, f32[]{:T(128)}, f32[]{:T(128)}) all-reduce(f32[]{:T(128)} %get-tuple-element.32, f32[]{:T(128)} %get-tuple-element.33, f32[]{:T(128)} %get-tuple-element.34), channel_id=1, replica_groups=mesh['seq_0'=4,'seq_1'=2,'seq_2'=8,'dp_0'=2,'dp_1'=2] {'seq_2'}, use_global_device_ids=true, to_apply=%region_3.4 | all-reduce | flops 3 | bytes 24 | tf_op jit(solution)/shard_map/psum | solution.py:40
  746.5 5.9 all-reduce.3
  752.4 11.5 %all-reduce.2 = (f32[]{:T(128)}, f32[]{:T(128)}, f32[]{:T(128)}) all-reduce(f32[]{:T(128)} %get-tuple-element.29, f32[]{:T(128)} %get-tuple-element.30, f32[]{:T(128)} %get-tuple-element.31), channel_id=1, replica_groups=mesh['seq_0'=4,'seq_1'=2,'seq_2'=8,'dp_0'=2,'dp_1'=2] {'dp_1'}, use_global_device_ids=true, to_apply=%region_5.6 | all-reduce | flops 3 | bytes 24 | tf_op jit(solution)/shard_map/psum | solution.py:40
  (71 shorter events, 57.4 us)
Async XLA Ops:
  7.2 23.9 %copy-start.4 = (bf16[1,256,2048]{2,1,0:T(8,128)(2,1)S(1)}, bf16[1,256,2048]{2,1,0:T(8,128)(2,1)}, u32[]{:S(2)}) copy-start(bf16[1,256,2048]{2,1,0:T(8,128)(2,1)} %param.6) | copy-start | bytes 3145732
  7.2 281.8 %all-gather.2.cloned.1.call-start = ((), (), s32[]{:S(2)}) async-start(), calls=%async_computation.2 | async-start | bytes 7454720 | tf_op jit(solution)/shard_map/all_gather | solution.py:92
  7.9 648.8 %reduce-scatter.2.cloned.1.call-start = ((), (), s32[]{:S(2)}) async-start(), calls=%async_computation.3 | async-start | bytes 14909440 | tf_op jit(solution)/shard_map/reduce_scatter | solution.py:125
  9.2 22.8 %collective-permute-start.3 = (bf16[256,1024]{0,1:T(8,128)(2,1)S(1)}, bf16[256,1024]{0,1:T(8,128)(2,1)}, u32[]{:S(2)}, u32[]{:S(2)}) collective-permute-start(bf16[256,1024]{0,1:T(8,128)(2,1)S(1)} %bitcast.113), channel_id=1, source_target_pairs={{0,4},{4,8},{8,12},{12,16},{16,20},{20,24},{24,28},{28,32},{32,36}... | collective-permute-start | bytes 1572872 | tf_op jit(solution)/shard_map/ppermute | solution.py:24
  14.4 28.2 %collective-permute-start.2 = (bf16[256,1024]{0,1:T(8,128)(2,1)S(1)}, bf16[256,1024]{0,1:T(8,128)(2,1)}, u32[]{:S(2)}, u32[]{:S(2)}) collective-permute-start(bf16[256,1024]{0,1:T(8,128)(2,1)S(1)} %bitcast.114), channel_id=1, source_target_pairs={{0,8},{4,12},{8,16},{12,20},{16,24},{20,28},{24,32},{28,36},{32,40... | collective-permute-start | bytes 1572872 | tf_op jit(solution)/shard_map/ppermute | solution.py:24
  20.5 46.9 %collective-permute-start.1 = (bf16[256,1024]{0,1:T(8,128)(2,1)S(1)}, bf16[256,1024]{0,1:T(8,128)(2,1)}, u32[]{:S(2)}, u32[]{:S(2)}) collective-permute-start(bf16[256,1024]{0,1:T(8,128)(2,1)S(1)} %bitcast.110), channel_id=1, source_target_pairs={{0,4},{4,8},{8,12},{12,16},{16,20},{20,24},{24,28},{28,32},{32,36}... | collective-permute-start | bytes 1572872 | tf_op jit(solution)/shard_map/ppermute | solution.py:24
  26.1 60.1 %collective-permute-start = (bf16[256,1024]{0,1:T(8,128)(2,1)S(1)}, bf16[256,1024]{0,1:T(8,128)(2,1)}, u32[]{:S(2)}, u32[]{:S(2)}) collective-permute-start(bf16[256,1024]{0,1:T(8,128)(2,1)S(1)} %bitcast.111), channel_id=1, source_target_pairs={{0,8},{4,12},{8,16},{12,20},{16,24},{20,28},{24,32},{28,36},{32,40... | collective-permute-start | bytes 1572872 | tf_op jit(solution)/shard_map/ppermute | solution.py:24
  31.6 57.8 %copy-start.1 = (bf16[1,256,2048]{1,2,0:T(8,128)(2,1)}, bf16[1,256,2048]{1,2,0:T(8,128)(2,1)S(1)}, u32[]{:S(2)}) copy-start(bf16[1,256,2048]{1,2,0:T(8,128)(2,1)S(1)} %copy.102) | copy-start | bytes 3145732
  31.6 55.8 %copy-start.6 = (bf16[256,4,256]{2,0,1:T(8,128)(2,1)S(1)}, bf16[256,4,256]{2,0,1:T(8,128)(2,1)}, u32[]{:S(2)}) copy-start(bf16[256,4,256]{2,0,1:T(8,128)(2,1)} %copy.59) | copy-start | bytes 1572868
  68.6 20.8 %copy-start.7 = (bf16[256,4,256]{2,0,1:T(8,128)(2,1)}, bf16[256,4,256]{2,0,1:T(8,128)(2,1)S(1)}, u32[]{:S(2)}) copy-start(bf16[256,4,256]{2,0,1:T(8,128)(2,1)S(1)} %copy.58) | copy-start | bytes 1572868
  87.4 2.0 copy-start.8
  89.4 2.6 copy-start
  305.6 3.2 copy-start.5
  319.8 6.9 copy-start.2
  326.7 2.6 copy-start.3
  334.5 379.7 %collective-permute-start.5 = (bf16[256,1024]{1,0:T(8,128)(2,1)}, bf16[256,1024]{1,0:T(8,128)(2,1)}, u32[]{:S(2)}, u32[]{:S(2)}) collective-permute-start(bf16[256,1024]{1,0:T(8,128)(2,1)} %copy.75), channel_id=1, source_target_pairs={{8,0},{12,4},{16,8},{20,12},{24,16},{28,20},{32,24},{36,28},{40,32... | collective-permute-start | bytes 1572872 | tf_op jit(solution)/shard_map/ppermute | solution.py:24
  335.8 378.4 %collective-permute-start.4 = (bf16[256,1024]{1,0:T(8,128)(2,1)}, bf16[256,1024]{1,0:T(8,128)(2,1)}, u32[]{:S(2)}, u32[]{:S(2)}) collective-permute-start(bf16[256,1024]{1,0:T(8,128)(2,1)} %copy.73), channel_id=1, source_target_pairs={{4,0},{8,4},{12,8},{16,12},{20,16},{24,20},{28,24},{32,28},{36,32}... | collective-permute-start | bytes 1572872 | tf_op jit(solution)/shard_map/ppermute | solution.py:24
  343.1 374.5 %collective-permute-start.7 = (bf16[256,1024]{1,0:T(8,128)(2,1)}, bf16[256,1024]{1,0:T(8,128)(2,1)}, u32[]{:S(2)}, u32[]{:S(2)}) collective-permute-start(bf16[256,1024]{1,0:T(8,128)(2,1)} %copy.80), channel_id=1, source_target_pairs={{8,0},{12,4},{16,8},{20,12},{24,16},{28,20},{32,24},{36,28},{40,32... | collective-permute-start | bytes 1572872 | tf_op jit(solution)/shard_map/ppermute | solution.py:24
  344.4 373.2 %collective-permute-start.6 = (bf16[256,1024]{1,0:T(8,128)(2,1)}, bf16[256,1024]{1,0:T(8,128)(2,1)}, u32[]{:S(2)}, u32[]{:S(2)}) collective-permute-start(bf16[256,1024]{1,0:T(8,128)(2,1)} %copy.78), channel_id=1, source_target_pairs={{4,0},{8,4},{12,8},{16,12},{20,16},{24,20},{28,24},{32,28},{36,32}... | collective-permute-start | bytes 1572872 | tf_op jit(solution)/shard_map/ppermute | solution.py:24
  658.4 64.4 %all-to-all-start = ((bf16[4,32,1792]{2,1,0:T(8,128)(2,1)}), bf16[4,32,1792]{2,1,0:T(8,128)(2,1)S(1)}, u32[]{:S(2)}, u32[]{:S(2)}) async-start(bf16[4,32,1792]{2,1,0:T(8,128)(2,1)} %broadcast_in_dim.53), calls=%async_computation.1 | async-start | bytes 917504 | tf_op jit(solution)/shard_map/all_to_all | solution.py:29
Sparse Core Ops, SparseCore 0:
  9.8 279.1 all-gather.1
  316.3 340.3 reduce-scatter.1
where the time goes:
time: 784 us; the launch traced here: 783 us
  waiting for transfers between devices  549 us (70%)
  starting transfers between devices  78.9 us (10%)
  blocking collectives  39.8 us (5%)
  matrix products  37.8 us (5%)
  local copies, waits for them, and re-layouts  37.5 us (5%)
  between operations  21.5 us (3%)
  other arithmetic  18.2 us (2%)
    reduce_scatter x1, waiting for transfers between devices, shards(): lax.psum_scatter(lax.dot_general(attn, masked, (((0,), (0,)), ((), ())),...  302 us
    all_gather x1, waiting for transfers between devices, shards(): lax.all_gather(out_weight, SEQ, axis=0, tiled=True)  195 us
    all_to_all x1, starting transfers between devices, copy_for_each(): lax.all_to_all(jnp.broadcast_to(value[None], (size, *value.shape)), axis,...  55.7 us
    ppermute x8, waiting for transfers between devices, shifted(): lax.ppermute(value, axis, [(source, source + steps) for source in range(i...  48.6 us
    psum x5, blocking collectives, over_axes(): return functools.reduce(lax.psum, axes, value)  39.8 us
    ppermute x8, starting transfers between devices, shifted(): lax.ppermute(value, axis, [(source, source + steps) for source in range(i...  23.1 us
  transfers between devices with their start and end apart: 11, of which 6 were waited for; matrix products, arithmetic and copies ran while one was open for 7% of the time, Pallas kernels for 0%

commit v1 on v0

--- a/solution.py
+++ b/solution.py
@@ -16,6 +16,11 @@
 SEQ_DP = ("seq_0", "seq_1", "seq_2", "dp_0", "dp_1")
 SCALE = 0.0625
 CAP = 50.0
+
+
+def gather_over(x, axis, dim):
+    sent = jnp.stack([x] * lax.axis_size(axis))
+    return jnp.concatenate(lax.all_to_all(sent, axis, 0, 0), axis=dim)
 
 
 def shifted(value, axis, steps):
@@ -89,7 +94,7 @@
     masked = jnp.where(valid[:, None], out_grad[0], jnp.zeros((), jnp.bfloat16))
     grad_attn = lax.dot_general(
         masked,
-        lax.all_gather(out_weight, SEQ, axis=0, tiled=True),
+        gather_over(out_weight, SEQ, 0),
         (((1,), (1,)), ((), ())),
         preferred_element_type=jnp.float32,
     ).astype(jnp.bfloat16)

time: 784 us -> 738 us (0.941)
  waiting for transfers between devices: 549 us -> 500 us
    all_gather x1 -> x0, waiting for transfers between devices: 195 us -> none  [shards(): lax.all_gather(out_weight, SEQ, axis=0, tiled=True)]
    ppermute x8, waiting for transfers between devices: 48.6 us -> 195 us  [shifted(): lax.ppermute(value, axis, [(source, source + steps) for source in range(i...]
    all_to_all x1, starting transfers between devices: 55.7 us -> 41.1 us  [copy_for_each(): lax.all_to_all(jnp.broadcast_to(value[None], (size, *value.shape)), axis,...]
    all_to_all x0 -> x1, starting transfers between devices: none -> 13.9 us  [gather_over(): return jnp.concatenate(lax.all_to_all(sent, axis, 0, 0), axis=dim)]
where the time goes in v1:
time: 738 us; the launch traced here: 736 us
  waiting for transfers between devices  500 us (68%)
  starting transfers between devices  75.1 us (10%)
  blocking collectives  42.2 us (6%)
  local copies, waits for them, and re-layouts  41 us (6%)
  matrix products  37.7 us (5%)
  between operations  21.5 us (3%)
  other arithmetic  18.2 us (2%)
    reduce_scatter x1, waiting for transfers between devices, shards(): lax.psum_scatter(lax.dot_general(attn, masked, (((0,), (0,)), ((), ())),...  303 us
    ppermute x8, waiting for transfers between devices, shifted(): lax.ppermute(value, axis, [(source, source + steps) for source in range(i...  195 us
    psum x5, blocking collectives, over_axes(): return functools.reduce(lax.psum, axes, value)  42.2 us
    all_to_all x1, starting transfers between devices, copy_for_each(): lax.all_to_all(jnp.broadcast_to(value[None], (size, *value.shape)), axis,...  41.1 us
    ppermute x8, starting transfers between devices, shifted(): lax.ppermute(value, axis, [(source, source + steps) for source in range(i...  20 us
  transfers between devices with their start and end apart: 11, of which 6 were waited for; matrix products, arithmetic and copies ran while one was open for 7% of the time, Pallas kernels for 0%

profile of v1, /device:TPU:1, one launch (start us, length us, event | category | flops | bytes accessed | tf_op | source)
XLA Modules:
  0.0 736.2 jit_solution(4632654878203520014)
XLA Ops:
  7.2 4.8 stack.2
  12.0 13.9 %all-to-all-start = ((bf16[64,32,1792]{2,1,0:T(8,128)(2,1)}), bf16[64,32,1792]{2,1,0:T(8,128)(2,1)}, u32[]{:S(2)}, u32[]{:S(2)}) async-start(bf16[64,32,1792]{2,1,0:T(8,128)(2,1)} %stack.2), calls=%async_computation | async-start | bytes 14680064 | tf_op jit(solution)/shard_map/all_to_all | solution.py:23
  26.2 3.7 collective-permute-start.1
  29.9 4.0 collective-permute-start
  34.1 5.1 collective-permute-start.3
  44.0 149.4 %collective-permute-done.1 = bf16[256,1024]{0,1:T(8,128)(2,1)} collective-permute-done((bf16[256,1024]{0,1:T(8,128)(2,1)S(1)}, bf16[256,1024]{0,1:T(8,128)(2,1)}, u32[]{:S(2)}, u32[]{:S(2)}) %collective-permute-start.1) | collective-permute-done | bytes 524320 | tf_op jit(solution)/shard_map/ppermute | solution.py:29
  194.7 15.3 %collective-permute-done = bf16[256,1024]{0,1:T(8,128)(2,1)} collective-permute-done((bf16[256,1024]{0,1:T(8,128)(2,1)S(1)}, bf16[256,1024]{0,1:T(8,128)(2,1)}, u32[]{:S(2)}, u32[]{:S(2)}) %collective-permute-start) | collective-permute-done | bytes 524320 | tf_op jit(solution)/shard_map/ppermute | solution.py:29
  211.2 15.9 %collective-permute-done.3 = bf16[256,1024]{0,1:T(8,128)(2,1)} collective-permute-done((bf16[256,1024]{0,1:T(8,128)(2,1)S(1)}, bf16[256,1024]{0,1:T(8,128)(2,1)}, u32[]{:S(2)}, u32[]{:S(2)}) %collective-permute-start.3) | collective-permute-done | bytes 524320 | tf_op jit(solution)/shard_map/ppermute | solution.py:29
  229.2 14.6 %collective-permute-done.2 = bf16[256,1024]{0,1:T(8,128)(2,1)} collective-permute-done((bf16[256,1024]{0,1:T(8,128)(2,1)S(1)}, bf16[256,1024]{0,1:T(8,128)(2,1)}, u32[]{:S(2)}, u32[]{:S(2)}) %collective-permute-start.2) | collective-permute-done | bytes 524320 | tf_op jit(solution)/shard_map/ppermute | solution.py:29
  252.2 6.5 convolution_convert_fusion
  261.3 3.3 bitcast_convert_fusion
  264.6 4.1 copy.91
  272.0 7.4 fusion.6
  279.3 3.6 copy.76
  283.0 6.8 fusion.1
  300.2 3.9 fusion.24
  313.9 5.4 multiply_reduce_fusion.1
  319.3 302.8 %reduce-scatter.2.cloned.1.call-done = f32[32,1792]{1,0:T(8,128)} async-done(((f32[2048,1792]{1,0:T(8,128)}), f32[32,1792]{1,0:T(8,128)}) %reduce-scatter.2.cloned.1.call-update) | async-done | bytes 229392 | tf_op jit(solution)/shard_map/reduce_scatter | solution.py:130
  623.8 41.1 %all-to-all-start.1 = ((bf16[4,32,1792]{2,1,0:T(8,128)(2,1)}), bf16[4,32,1792]{2,1,0:T(8,128)(2,1)S(1)}, u32[]{:S(2)}, u32[]{:S(2)}) async-start(bf16[4,32,1792]{2,1,0:T(8,128)(2,1)} %broadcast_in_dim.47), calls=%async_computation.2 | async-start | bytes 917504 | tf_op jit(solution)/shard_map/all_to_all | solution.py:34
  674.9 6.5 all-reduce.1
  681.5 4.4 all-reduce.4
  685.9 13.9 %all-reduce = (f32[]{:T(128)}, f32[]{:T(128)}, f32[]{:T(128)}) all-reduce(f32[]{:T(128)} %get-tuple-element.32, f32[]{:T(128)} %get-tuple-element.33, f32[]{:T(128)} %get-tuple-element.34), channel_id=1, replica_groups=mesh['seq_0'=4,'seq_1'=2,'seq_2'=8,'dp_0'=2,'dp_1'=2] {'seq_2'}, use_global_device_ids=true, to_apply=%region_3.4 | all-reduce | flops 3 | bytes 24 | tf_op jit(solution)/shard_map/psum | solution.py:45
  699.8 5.9 all-reduce.3
  705.7 11.5 %all-reduce.2 = (f32[]{:T(128)}, f32[]{:T(128)}, f32[]{:T(128)}) all-reduce(f32[]{:T(128)} %get-tuple-element.29, f32[]{:T(128)} %get-tuple-element.30, f32[]{:T(128)} %get-tuple-element.31), channel_id=1, replica_groups=mesh['seq_0'=4,'seq_1'=2,'seq_2'=8,'dp_0'=2,'dp_1'=2] {'dp_1'}, use_global_device_ids=true, to_apply=%region_5.6 | all-reduce | flops 3 | bytes 24 | tf_op jit(solution)/shard_map/psum | solution.py:45
  (77 shorter events, 60.9 us)
Async XLA Ops:
  12.0 14.0 %copy-start.7 = (bf16[1,256,1024]{2,1,0:T(8,128)(2,1)S(1)}, bf16[1,256,1024]{2,1,0:T(8,128)(2,1)}, u32[]{:S(2)}) copy-start(bf16[1,256,1024]{2,1,0:T(8,128)(2,1)} %param.7) | copy-start | bytes 1572868
  12.0 21.9 %copy-start.8 = (bf16[1,256,1024]{2,1,0:T(8,128)(2,1)S(1)}, bf16[1,256,1024]{2,1,0:T(8,128)(2,1)}, u32[]{:S(2)}) copy-start(bf16[1,256,1024]{2,1,0:T(8,128)(2,1)} %param.8) | copy-start | bytes 1572868
  12.0 29.3 %copy-start.5 = (bf16[1,256,2048]{2,1,0:T(8,128)(2,1)S(1)}, bf16[1,256,2048]{2,1,0:T(8,128)(2,1)}, u32[]{:S(2)}) copy-start(bf16[1,256,2048]{2,1,0:T(8,128)(2,1)} %param.6) | copy-start | bytes 3145732
  12.0 240.2 %all-to-all-start = ((bf16[64,32,1792]{2,1,0:T(8,128)(2,1)}), bf16[64,32,1792]{2,1,0:T(8,128)(2,1)}, u32[]{:S(2)}, u32[]{:S(2)}) async-start(bf16[64,32,1792]{2,1,0:T(8,128)(2,1)} %stack.2), calls=%async_computation | async-start | bytes 14680064 | tf_op jit(solution)/shard_map/all_to_all | solution.py:23
  25.9 596.1 %reduce-scatter.2.cloned.1.call-start = ((), (), s32[]{:S(2)}) async-start(), calls=%async_computation.3 | async-start | bytes 14909440 | tf_op jit(solution)/shard_map/reduce_scatter | solution.py:130
  26.2 167.2 %collective-permute-start.1 = (bf16[256,1024]{0,1:T(8,128)(2,1)S(1)}, bf16[256,1024]{0,1:T(8,128)(2,1)}, u32[]{:S(2)}, u32[]{:S(2)}) collective-permute-start(bf16[256,1024]{0,1:T(8,128)(2,1)S(1)} %bitcast.113), channel_id=1, source_target_pairs={{0,4},{4,8},{8,12},{12,16},{16,20},{20,24},{24,28},{28,32},{32,36}... | collective-permute-start | bytes 1572872 | tf_op jit(solution)/shard_map/ppermute | solution.py:29
  29.9 180.1 %collective-permute-start = (bf16[256,1024]{0,1:T(8,128)(2,1)S(1)}, bf16[256,1024]{0,1:T(8,128)(2,1)}, u32[]{:S(2)}, u32[]{:S(2)}) collective-permute-start(bf16[256,1024]{0,1:T(8,128)(2,1)S(1)} %bitcast.114), channel_id=1, source_target_pairs={{0,8},{4,12},{8,16},{12,20},{16,24},{20,28},{24,32},{28,36},{32,40... | collective-permute-start | bytes 1572872 | tf_op jit(solution)/shard_map/ppermute | solution.py:29
  34.1 193.1 %collective-permute-start.3 = (bf16[256,1024]{0,1:T(8,128)(2,1)S(1)}, bf16[256,1024]{0,1:T(8,128)(2,1)}, u32[]{:S(2)}, u32[]{:S(2)}) collective-permute-start(bf16[256,1024]{0,1:T(8,128)(2,1)S(1)} %bitcast.110), channel_id=1, source_target_pairs={{0,4},{4,8},{8,12},{12,16},{16,20},{20,24},{24,28},{28,32},{32,36}... | collective-permute-start | bytes 1572872 | tf_op jit(solution)/shard_map/ppermute | solution.py:29
  39.2 204.6 %collective-permute-start.2 = (bf16[256,1024]{0,1:T(8,128)(2,1)S(1)}, bf16[256,1024]{0,1:T(8,128)(2,1)}, u32[]{:S(2)}, u32[]{:S(2)}) collective-permute-start(bf16[256,1024]{0,1:T(8,128)(2,1)S(1)} %bitcast.111), channel_id=1, source_target_pairs={{0,8},{4,12},{8,16},{12,20},{16,24},{20,28},{24,32},{28,36},{32,40... | collective-permute-start | bytes 1572872 | tf_op jit(solution)/shard_map/ppermute | solution.py:29
  41.8 204.0 %copy-start.1 = (bf16[1,256,2048]{1,2,0:T(8,128)(2,1)}, bf16[1,256,2048]{1,2,0:T(8,128)(2,1)S(1)}, u32[]{:S(2)}) copy-start(bf16[1,256,2048]{1,2,0:T(8,128)(2,1)S(1)} %copy.102) | copy-start | bytes 3145732
  42.0 205.8 %copy-start.9 = (bf16[256,4,256]{2,0,1:T(8,128)(2,1)}, bf16[256,4,256]{2,0,1:T(8,128)(2,1)S(1)}, u32[]{:S(2)}) copy-start(bf16[256,4,256]{2,0,1:T(8,128)(2,1)S(1)} %copy.59) | copy-start | bytes 1572868
  194.7 53.1 %copy-start.10 = (bf16[256,4,256]{2,0,1:T(8,128)(2,1)}, bf16[256,4,256]{2,0,1:T(8,128)(2,1)S(1)}, u32[]{:S(2)}) copy-start(bf16[256,4,256]{2,0,1:T(8,128)(2,1)S(1)} %copy.58) | copy-start | bytes 1572868
  211.2 36.6 %copy-start.11 = (bf16[256,4,256]{2,0,1:T(8,128)(2,1)}, bf16[256,4,256]{2,0,1:T(8,128)(2,1)S(1)}, u32[]{:S(2)}) copy-start(bf16[256,4,256]{2,0,1:T(8,128)(2,1)S(1)} %copy.57) | copy-start | bytes 1572868
  247.8 2.6 copy-start
  268.7 3.2 copy-start.6
  283.0 6.9 copy-start.2
  289.9 2.6 copy-start.3
  295.6 369.3 %collective-permute-start.5 = (bf16[256,1024]{1,0:T(8,128)(2,1)}, bf16[256,1024]{1,0:T(8,128)(2,1)}, u32[]{:S(2)}, u32[]{:S(2)}) collective-permute-start(bf16[256,1024]{1,0:T(8,128)(2,1)} %copy.75), channel_id=1, source_target_pairs={{8,0},{12,4},{16,8},{20,12},{24,16},{28,20},{32,24},{36,28},{40,32... | collective-permute-start | bytes 1572872 | tf_op jit(solution)/shard_map/ppermute | solution.py:29
  298.9 366.0 %collective-permute-start.4 = (bf16[256,1024]{1,0:T(8,128)(2,1)}, bf16[256,1024]{1,0:T(8,128)(2,1)}, u32[]{:S(2)}, u32[]{:S(2)}) collective-permute-start(bf16[256,1024]{1,0:T(8,128)(2,1)} %copy.73), channel_id=1, source_target_pairs={{4,0},{8,4},{12,8},{16,12},{20,16},{24,20},{28,24},{32,28},{36,32}... | collective-permute-start | bytes 1572872 | tf_op jit(solution)/shard_map/ppermute | solution.py:29
  307.6 360.7 %collective-permute-start.7 = (bf16[256,1024]{1,0:T(8,128)(2,1)}, bf16[256,1024]{1,0:T(8,128)(2,1)}, u32[]{:S(2)}, u32[]{:S(2)}) collective-permute-start(bf16[256,1024]{1,0:T(8,128)(2,1)} %copy.80), channel_id=1, source_target_pairs={{8,0},{12,4},{16,8},{20,12},{24,16},{28,20},{32,24},{36,28},{40,32... | collective-permute-start | bytes 1572872 | tf_op jit(solution)/shard_map/ppermute | solution.py:29
  312.6 355.7 %collective-permute-start.6 = (bf16[256,1024]{1,0:T(8,128)(2,1)}, bf16[256,1024]{1,0:T(8,128)(2,1)S(1)}, u32[]{:S(2)}, u32[]{:S(2)}) collective-permute-start(bf16[256,1024]{1,0:T(8,128)(2,1)} %copy.78), channel_id=1, source_target_pairs={{4,0},{8,4},{12,8},{16,12},{20,16},{24,20},{28,24},{32,28},{36,32}... | collective-permute-start | bytes 1572872 | tf_op jit(solution)/shard_map/ppermute | solution.py:29
  623.8 49.8 %all-to-all-start.1 = ((bf16[4,32,1792]{2,1,0:T(8,128)(2,1)}), bf16[4,32,1792]{2,1,0:T(8,128)(2,1)S(1)}, u32[]{:S(2)}, u32[]{:S(2)}) async-start(bf16[4,32,1792]{2,1,0:T(8,128)(2,1)} %broadcast_in_dim.47), calls=%async_computation.2 | async-start | bytes 917504 | tf_op jit(solution)/shard_map/all_to_all | solution.py:34
  668.3 50.9 %copy-start.4 = (bf16[256,1024]{1,0:T(8,128)(2,1)}, bf16[256,1024]{1,0:T(8,128)(2,1)S(1)}, u32[]{:S(2)}) copy-start(bf16[256,1024]{1,0:T(8,128)(2,1)S(1)} %collective-permute-done.6) | copy-start | bytes 1572868
Sparse Core Ops, SparseCore 0:
  279.5 342.5 reduce-scatter.1
